TPU v7x, 256 devices: a whole 4x4x8 slice. The times are simulated.
256 devices in a mesh: img: 16 (over y, x), row: 16 (over z, core).
Axes of the slice: x: 4, y: 4, z: 8, core: 2. Of those that a mesh axis runs over, the one named last changes fastest.
Arguments:
- latent: bfloat16 [1024, 128, 512], P(('img', 'row')), parts along dimension 0, may hold values from -8 to 8
- attn_gain: float32 [512], replicated, may hold values from 0.5 to 1.5
- attn_shift: float32 [512], replicated, may hold values from -3 to 3
- w_query: bfloat16 [512, 512], replicated, may hold values from -2 to 2
- w_key: bfloat16 [512, 512], replicated, may hold values from -2 to 2
- w_value: bfloat16 [512, 512], replicated, may hold values from -0.25 to 0.25
- w_out: bfloat16 [512, 512], replicated, may hold values from -0.25 to 0.25
- conv_gain: float32 [512], replicated, may hold values from 0.5 to 1.5
- conv_shift: float32 [512], replicated, may hold values from -3 to 3
- w_conv: bfloat16 [3, 3, 512, 512], replicated, may hold values from -0.09375 to 0.09375
- conv_bias: float32 [512], replicated, may hold values from -3 to 3
Outputs:
- encoded: bfloat16 [1024, 128, 512], P(('img', 'row')), parts along dimension 0
There are 16 independent parts, one for each index of `img`. A program takes and returns all parts, laid end to end along the dimension named above; an argument that names none is the same for every part. Nothing has to cross between parts.
All inputs are finite; a program needn't handle non-finite values.
Results may differ from a plain program's by a relative error of at most 0.011.
Values may be sent and summed in bfloat16 or wider, within the bound.
No kernel may reach another device: no remote copies, remote signals or barrier semaphores. Data moves between devices by JAX's collectives and lax.ppermute only.
A program may use at most 128 MiB of HBM per device.

v0:
```python
import jax
import jax.numpy as jnp
from jax import lax
from jax.sharding import PartitionSpec as P

C = 512
GROUPS = 32
W = 128
epsilon = 1e-06


def copy_for_each(shard, axis):
    copies = jnp.broadcast_to(shard, (lax.axis_size(axis), *shard.shape))
    return lax.all_to_all(copies, axis, split_axis=0, concat_axis=0, tiled=True)


def taken_together(shard, axis):
    return copy_for_each(shard, axis).sum(axis=0)


def together(arrays, axis):
    line, at, done = (jnp.concatenate([a.reshape(-1) for a in arrays]), 0, [])
    total = taken_together(line, axis)
    for a in arrays:
        done.append(total[at : at + a.size].reshape(a.shape))
        at += a.size
    return tuple(done)


def with_halo(cells, sides, width):
    for axis, dim in sides:
        count = lax.axis_size(axis)
        ends = count - 1
        head = lax.slice_in_dim(cells, 0, width, axis=dim)
        tail = lax.slice_in_dim(cells, cells.shape[dim] - width, cells.shape[dim], axis=dim)
        cells = jnp.concatenate(
            [
                lax.ppermute(tail, axis, [(i, (i + 1) % count) for i in range(ends)]),
                cells,
                lax.ppermute(head, axis, [((i + 1) % count, i) for i in range(ends)]),
            ],
            axis=dim,
        )
    return cells


def group_stats(grouped, count):
    first, second = together(
        (jnp.sum(grouped, axis=(0, 2)), jnp.sum(grouped * grouped, axis=(0, 2))), "row"
    )
    centre = first / count
    spread = second / count - centre * centre
    return (centre, spread)


def group_norm(field, gain, shift):
    grouped = field.reshape(field.shape[0], GROUPS, C // GROUPS)
    count = field.shape[0] * lax.axis_size("row") * (C // GROUPS)
    centre, spread = group_stats(grouped, count)
    normed = (grouped - centre[None, :, None]) * lax.rsqrt(spread + epsilon)[None, :, None]
    return normed.reshape(field.shape) * gain + shift


def attend(carry, key_piece, value_piece, queries):
    maxima, denominator, accumulated = carry
    scaling = 1.0 / jnp.sqrt(jnp.float32(C))
    scores = (
        jnp.einsum("qc,kc->qk", queries, key_piece, preferred_element_type=jnp.float32) * scaling
    )
    newest = jnp.maximum(maxima, jnp.max(scores, axis=1))
    expo = jnp.exp(scores - newest[:, None])
    denominator = jnp.sum(expo, axis=1)
    accumulated = jnp.dot(
        expo.astype(jnp.bfloat16), value_piece, preferred_element_type=jnp.float32
    )
    return (newest, denominator, accumulated)


def local(
    latent,
    attn_gain,
    attn_shift,
    w_query,
    w_key,
    w_value,
    w_out,
    conv_gain,
    conv_shift,
    w_conv,
    conv_bias,
):
    local_rows = latent.shape[0]
    positions = latent.reshape(local_rows * W, C)
    normed = group_norm(positions.astype(jnp.float32), attn_gain, attn_shift).astype(jnp.bfloat16)
    queries = jnp.dot(normed, w_query, preferred_element_type=jnp.float32).astype(jnp.bfloat16)
    count_rows = positions.shape[0]
    start_carry = (
        jnp.full((count_rows,), -1e30, jnp.float32),
        jnp.zeros((count_rows,), jnp.float32),
        jnp.zeros((count_rows, C), jnp.float32),
    )
    piece = lax.all_gather(normed, "row", axis=0, tiled=True)
    key_piece = jnp.dot(piece, w_key, preferred_element_type=jnp.float32).astype(jnp.bfloat16)
    value_piece = jnp.dot(piece, w_value, preferred_element_type=jnp.float32).astype(jnp.bfloat16)
    maxima, denominator, accumulated = attend(start_carry, key_piece, value_piece, queries)
    attended = (accumulated / denominator[:, None]).astype(jnp.bfloat16)
    hidden = (
        positions.astype(jnp.float32) + jnp.dot(attended, w_out, preferred_element_type=jnp.float32)
    ).astype(jnp.bfloat16)
    activated = jax.nn.silu(group_norm(hidden.astype(jnp.float32), conv_gain, conv_shift)).astype(
        jnp.bfloat16
    )
    activated = activated.reshape(local_rows, W, C)
    bordered = with_halo(activated, (("row", 0),), 1)
    padded = jnp.pad(bordered, ((0, 0), (1, 1), (0, 0)))
    convolved = jnp.zeros((local_rows * W, C), jnp.float32)
    for row_tap in range(3):
        for col_tap in range(3):
            window = padded[row_tap : row_tap + local_rows, col_tap : col_tap + W].reshape(
                local_rows * W, C
            )
            convolved = convolved + jnp.dot(
                window, w_conv[row_tap, col_tap], preferred_element_type=jnp.float32
            )
    encoded = hidden.astype(jnp.float32) + (convolved + conv_bias)
    return encoded.astype(jnp.bfloat16).reshape(local_rows, W, C)


def solution(mesh):
    in_specs = (P(("img", "row"), None, None), P(), P(), P(), P(), P(), P(), P(), P(), P(), P())
    out_specs = P(("img", "row"), None, None)
    return jax.shard_map(local, mesh=mesh, in_specs=in_specs, out_specs=out_specs, check_vma=False)
```

profile of v0, /device:TPU:1, one launch (start us, length us, event | category | flops | bytes accessed | tf_op | source)
XLA Modules:
  0.0 157.1 jit_solution(7887998248014053439)
XLA Ops:
  6.5 1.3 convert_reduce_fusion.1
  8.0 0.1 reduce_sum.75
  8.1 0.1 reduce_sum.96
  8.3 16.8 %all_to_all.12 = f32[16,1,64]{2,1,0:T(1,128)S(1)} all-to-all(f32[16,1,64]{2,1,0:T(1,128)S(1)} %broadcast_in_dim.6), channel_id=1, replica_groups=mesh['img'=16,'row'=16] {'row'}, dimensions={0} | all-to-all | bytes 8192 | tf_op jit(solution)/shard_map/all_to_all | solution.py:14
  25.3 0.1 sub.41
  25.5 2.1 %fusion.31 = bf16[512,512]{1,0:T(8,128)(2,1)} fusion(bf16[4,128,512]{2,1,0:T(8,128)(2,1)} %param.11, f32[512]{0:T(512)} %param.13, f32[512]{0:T(512)} %param.12, f32[512]{0:T(512)S(1)} %mul.69, f32[512]{0:T(512)S(1)} %sub.41), kind=kLoop, calls=%fused_computation.46 | loop fusion | flops 1572864 | bytes 1056768 | tf_op jit(solution)/shard_map/convert_element_type | solution.py:94
  27.6 1.6 %convolution_convert_fusion.2 = bf16[512,512]{1,0:T(8,128)(2,1)S(1)} fusion(bf16[512,512]{1,0:T(8,128)(2,1)} %fusion.31, bf16[512,512]{1,0:T(8,128)(2,1)} %param.14), kind=kOutput, calls=%fused_computation.28 | convolution fusion | flops 268697600 | bytes 1572864 | tf_op jit(solution)/shard_map/dot_general | solution.py:95
  29.2 51.1 %all-gather.2.cloned.1.call-done = bf16[8192,512]{1,0:T(8,128)(2,1)} async-done(((bf16[512,512]{1,0:T(8,128)(2,1)}), bf16[8192,512]{1,0:T(8,128)(2,1)}) %all-gather.2.cloned.1.call-update) | async-done | bytes 8388624 | tf_op jit(solution)/shard_map/all_gather | solution.py:102
  80.4 14.5 %multiply_reduce_fusion = (f32[512]{0:T(512)S(1)}, f32[512,8192]{1,0:T(8,128)}) fusion(bf16[512,512]{1,0:T(8,128)(2,1)S(1)} %convolution_convert_fusion.2, bf16[8192,512]{1,0:T(8,128)(2,1)} %all-gather.2.cloned.1.call-done, bf16[512,512]{1,0:T(8,128)(2,1)S(1)} %copy-done), kind=kOutput, calls=%fused_computation.1 | convolution fusion | flops 8602517504 | bytes 26216448 | tf_op jit(solution)/shard_map/qc,kc->qk/dot_general | solution.py:68
  94.9 8.7 %fusion = f32[512]{0:T(512)S(1)} fusion(f32[512,8192]{1,0:T(8,128)} %get-tuple-element.24, f32[512]{0:T(512)S(1)} %broadcast_maximum_fusion), kind=kLoop, calls=%fused_computation.2 | loop fusion | flops 12582400 | bytes 16781312 | tf_op jit(solution)/shard_map/reduce_sum | solution.py:72
  103.6 17.2 %fusion.15 = bf16[512,512]{1,0:T(8,128)(2,1)S(1)} fusion(bf16[8192,512]{1,0:T(8,128)(2,1)} %all-gather.2.cloned.1.call-done, bf16[512,512]{1,0:T(8,128)(2,1)S(1)} %copy-done.5, f32[512,8192]{1,0:T(8,128)} %get-tuple-element.24, f32[512]{0:T(512)S(1)} %broadcast_maximum_fusion, f32[512]{0:T(512)S(1)} %fusion), kind=kOutput, calls=%fused_computation.31 | convolution fusion | flops 8607236096 | bytes 26218496 | tf_op jit(solution)/shard_map/dot_general | solution.py:73
  120.8 0.5 convert_reduce_fusion
  121.4 0.3 reduce_sum.101
  121.8 0.1 reduce_sum.104
  122.0 11.4 %all_to_all.13 = f32[16,1,64]{2,1,0:T(1,128)S(1)} all-to-all(f32[16,1,64]{2,1,0:T(1,128)S(1)} %broadcast_in_dim.8), channel_id=1, replica_groups=mesh['img'=16,'row'=16] {'row'}, dimensions={0} | all-to-all | bytes 8192 | tf_op jit(solution)/shard_map/all_to_all | solution.py:14
  133.8 0.4 fusion.27
  134.2 2.7 %collective-permute-start = (bf16[1,128,512]{2,1,0:T(8,128)(2,1)S(1)}, bf16[1,128,512]{2,1,0:T(8,128)(2,1)S(1)}, u32[]{:S(2)}, u32[]{:S(2)}) collective-permute-start(bf16[1,128,512]{2,1,0:T(8,128)(2,1)S(1)} %get-tuple-element.17), channel_id=1, source_target_pairs={{0,1},{1,2},{2,3},{3,4},{4,5},{5,6},{6,7},{7,8},{8,9},{9,10},{10,1... | collective-permute-start | bytes 393224 | tf_op jit(solution)/shard_map/ppermute | solution.py:38
  137.0 1.9 %collective-permute-start.1 = (bf16[1,128,512]{2,1,0:T(8,128)(2,1)S(1)}, bf16[1,128,512]{2,1,0:T(8,128)(2,1)S(1)}, u32[]{:S(2)}, u32[]{:S(2)}) collective-permute-start(bf16[1,128,512]{2,1,0:T(8,128)(2,1)S(1)} %get-tuple-element.18), channel_id=1, source_target_pairs={{1,0},{2,1},{3,2},{4,3},{5,4},{6,5},{7,6},{8,7},{9,8},{10,9},{11,1... | collective-permute-start | bytes 393224 | tf_op jit(solution)/shard_map/ppermute | solution.py:40
  138.9 4.3 %collective-permute-done.1 = bf16[1,128,512]{2,1,0:T(8,128)(2,1)S(1)} collective-permute-done((bf16[1,128,512]{2,1,0:T(8,128)(2,1)S(1)}, bf16[1,128,512]{2,1,0:T(8,128)(2,1)S(1)}, u32[]{:S(2)}, u32[]{:S(2)}) %collective-permute-start.1) | collective-permute-done | bytes 131104 | tf_op jit(solution)/shard_map/ppermute | solution.py:40
  143.3 0.2 fusion.36
  143.5 0.4 fusion.58
  143.9 1.7 %fusion.46 = f32[512,512]{1,0:T(8,128)S(1)} fusion(bf16[512,512]{1,0:T(8,128)(2,1)S(1)} %bitcast.82, bf16[3,3,512,512]{3,2,1,0:T(8,128)(2,1)} %param.20), kind=kOutput, calls=%fused_computation.65 | convolution fusion | flops 268435456 | bytes 2097152 | tf_op jit(solution)/shard_map/dot_general | solution.py:122
  145.6 0.1 pad_maximum_fusion
  145.7 0.1 slice-done.1
  145.8 0.4 convolution_add_fusion.6
  146.3 0.4 convolution_add_fusion.5
  146.7 0.4 convolution_add_fusion.4
  147.2 0.4 convolution_add_fusion.3
  147.6 0.4 fusion.37
  148.1 0.4 convolution_add_fusion.2
  148.5 0.4 convolution_add_fusion.1
  149.0 1.3 fusion.10
  (42 shorter events, 1.3 us)
Async XLA Ops:
  6.5 73.8 %copy-start = (bf16[512,512]{1,0:T(8,128)(2,1)S(1)}, bf16[512,512]{1,0:T(8,128)(2,1)}, u32[]{:S(2)}) copy-start(bf16[512,512]{1,0:T(8,128)(2,1)} %param.15) | copy-start | bytes 1572868
  6.5 73.8 %all-gather.2.cloned.1.call-start = ((), (), s32[]{:S(2)}) async-start(), calls=%async_computation.2 | async-start | bytes 8912896 | tf_op jit(solution)/shard_map/all_gather | solution.py:102
  94.9 8.7 %copy-start.5 = (bf16[512,512]{1,0:T(8,128)(2,1)S(1)}, bf16[512,512]{1,0:T(8,128)(2,1)}, u32[]{:S(2)}) copy-start(bf16[512,512]{1,0:T(8,128)(2,1)} %param.16) | copy-start | bytes 1572868
  103.6 17.2 %copy-start.1 = (bf16[4,128,512]{2,1,0:T(8,128)(2,1)S(1)}, bf16[4,128,512]{2,1,0:T(8,128)(2,1)}, u32[]{:S(2)}) copy-start(bf16[4,128,512]{2,1,0:T(8,128)(2,1)} %param.11) | copy-start | bytes 1572868
  103.6 17.2 %copy-start.6 = (bf16[512,512]{1,0:T(8,128)(2,1)S(1)}, bf16[512,512]{1,0:T(8,128)(2,1)}, u32[]{:S(2)}) copy-start(bf16[512,512]{1,0:T(8,128)(2,1)} %param.17) | copy-start | bytes 1572868
  103.6 30.2 %copy-start.2 = (f32[512]{0:T(512)S(1)}, f32[512]{0:T(512)}, u32[]{:S(2)}) copy-start(f32[512]{0:T(512)} %param.19) | copy-start | bytes 6148
  103.6 30.2 %copy-start.3 = (f32[512]{0:T(512)S(1)}, f32[512]{0:T(512)}, u32[]{:S(2)}) copy-start(f32[512]{0:T(512)} %param.18) | copy-start | bytes 6148
  120.8 24.9 %slice-start = ((s8[4718592]{0:T(1024)(128)(4,1)}), s8[524288]{0:T(1024)(128)(4,1)S(1)}, s32[]{:S(2)}) async-start(s8[4718592]{0:T(1024)(128)(4,1)} %bitcast.74), calls=%async_computation.3 | async-start | bytes 1048576
  134.2 4.7 %collective-permute-start = (bf16[1,128,512]{2,1,0:T(8,128)(2,1)S(1)}, bf16[1,128,512]{2,1,0:T(8,128)(2,1)S(1)}, u32[]{:S(2)}, u32[]{:S(2)}) collective-permute-start(bf16[1,128,512]{2,1,0:T(8,128)(2,1)S(1)} %get-tuple-element.17), channel_id=1, source_target_pairs={{0,1},{1,2},{2,3},{3,4},{4,5},{5,6},{6,7},{7,8},{8,9},{9,10},{10,1... | collective-permute-start | bytes 393224 | tf_op jit(solution)/shard_map/ppermute | solution.py:38
  137.0 6.3 %collective-permute-start.1 = (bf16[1,128,512]{2,1,0:T(8,128)(2,1)S(1)}, bf16[1,128,512]{2,1,0:T(8,128)(2,1)S(1)}, u32[]{:S(2)}, u32[]{:S(2)}) collective-permute-start(bf16[1,128,512]{2,1,0:T(8,128)(2,1)S(1)} %get-tuple-element.18), channel_id=1, source_target_pairs={{1,0},{2,1},{3,2},{4,3},{5,4},{6,5},{7,6},{8,7},{9,8},{10,9},{11,1... | collective-permute-start | bytes 393224 | tf_op jit(solution)/shard_map/ppermute | solution.py:40
  143.5 2.3 %slice-start.1 = ((s8[4718592]{0:T(1024)(128)(4,1)}), s8[4194304]{0:T(1024)(128)(4,1)S(1)}, s32[]{:S(2)}) async-start(s8[4718592]{0:T(1024)(128)(4,1)} %bitcast.74), calls=%async_computation.4 | async-start | bytes 8388608
  146.3 2.7 %copy-start.4 = (f32[512]{0:T(512)S(1)}, f32[512]{0:T(512)}, u32[]{:S(2)}) copy-start(f32[512]{0:T(512)} %param.21) | copy-start | bytes 6148
Sparse Core Ops, SparseCore 0:
  27.7 52.6 all-gather.1
where the time goes:
time: 157 us
  waiting for transfers between devices  55.5 us (35%)
  matrix products  39.9 us (25%)
  blocking collectives  28.2 us (18%)
  other arithmetic  13.7 us (9%)
  between operations  13.6 us (9%)
  starting transfers between devices  4.64 us (3%)
    all_gather x1, waiting for transfers between devices, local(): piece = lax.all_gather(normed, 'row', axis=0, tiled=True)  51.1 us
    all_to_all x2, blocking collectives, copy_for_each(): return lax.all_to_all(copies, axis, split_axis=0, concat_axis=0, tiled=True)  28.2 us
    dot_general x1, matrix products, attend(): jnp.dot(expo.astype(jnp.bfloat16), value_piece, preferred_element_type=jn...  17.2 us
    dot_general x1, matrix products, attend(): jnp.einsum('qc,kc->qk', queries, key_piece, preferred_element_type=jnp.fl...  14.5 us
    reduce_sum x1, other arithmetic, attend(): denominator = jnp.sum(expo, axis=1)  8.68 us
    dot_general x9, matrix products, local(): jnp.dot(window, w_conv[row_tap, col_tap], preferred_element_type=jnp.floa...  6.07 us
    ppermute x1, waiting for transfers between devices, with_halo(): lax.ppermute(head, axis, [((i + 1) % count, i) for i in range(ends)])  4.35 us
  transfers between devices with their start and end apart: 3, of which 2 were waited for; matrix products, arithmetic and copies ran while one was open for 1% of the time, Pallas kernels for 0%

commit v1 on v0

--- a/solution.py
+++ b/solution.py
@@ -99,7 +99,19 @@
         jnp.zeros((count_rows,), jnp.float32),
         jnp.zeros((count_rows, C), jnp.float32),
     )
-    piece = lax.all_gather(normed, "row", axis=0, tiled=True)
+    slots = lax.axis_size("row")
+    pile = [(d, (d + 1) % slots) for d in range(slots)]
+    xs_all = [(d, (d - 1) % slots) for d in range(slots)]
+    t1, u1 = ([normed], [normed])
+    for _ in range(slots // 2):
+        reached = lax.ppermute(t1[-1], axis_name="row", perm=pile)
+        t1.append(reached)
+    for _ in range((slots - 1) // 2):
+        z_new = lax.ppermute(u1[-1], axis_name="row", perm=xs_all)
+        u1.append(z_new)
+    z2 = jnp.concatenate([*t1[::-1], *u1[1:]], 0)
+    arr_now = lax.axis_index("row")
+    piece = jnp.roll(z2, (arr_now - slots // 2) * normed.shape[0], 0)
     key_piece = jnp.dot(piece, w_key, preferred_element_type=jnp.float32).astype(jnp.bfloat16)
     value_piece = jnp.dot(piece, w_value, preferred_element_type=jnp.float32).astype(jnp.bfloat16)
     maxima, denominator, accumulated = attend(start_carry, key_piece, value_piece, queries)

time: 157 us -> 208 us (1.32)
  starting transfers between devices: 4.64 us -> 47.3 us
  local copies, waits for them, and re-layouts: 1.52 us -> 43.8 us
  waiting for transfers between devices: 55.5 us -> 30.4 us
  between operations: 13.6 us -> 0.33 us
  blocking collectives: 28.2 us -> 33.9 us
    all_gather x1 -> x0, waiting for transfers between devices: 51.1 us -> none  [local(): piece = lax.all_gather(normed, 'row', axis=0, tiled=True)]
    ppermute x0 -> x15, starting transfers between devices: none -> 42.7 us  [the longest x7 28.1 us: local(): z_new = lax.ppermute(u1[-1], axis_name='row', perm=xs_all)]
    unnamed x18 -> x73, local copies, waits for them, and re-layouts: 0.16 us -> 41.6 us
    ppermute x0 -> x15, waiting for transfers between devices: none -> 26 us  [the longest x8 20.5 us: local(): reached = lax.ppermute(t1[-1], axis_name='row', perm=pile)]
    all_to_all x2, blocking collectives: 28.2 us -> 33.9 us  [copy_for_each(): return lax.all_to_all(copies, axis, split_axis=0, concat_axis=0, tiled=True)]
    dot_general x1, matrix products: 17.2 us -> 14.2 us  [attend(): jnp.dot(expo.astype(jnp.bfloat16), value_piece, preferred_element_type=jn...]
  transfers between devices with their start and end apart: 3 -> 17, of which waited for: 2 -> 14; matrix products, arithmetic and copies ran while one was open for 1% -> 12% of each run, Pallas kernels for 0% -> 0%
where the time goes in v1:
time: 208 us
  starting transfers between devices  47.3 us (23%)
  local copies, waits for them, and re-layouts  43.8 us (21%)
  matrix products  39 us (19%)
  blocking collectives  33.9 us (16%)
  waiting for transfers between devices  30.4 us (15%)
  other arithmetic  12.7 us (6%)
    unnamed x73, local copies, waits for them, and re-layouts  41.6 us
    all_to_all x2, blocking collectives, copy_for_each(): return lax.all_to_all(copies, axis, split_axis=0, concat_axis=0, tiled=True)  33.9 us
    ppermute x7, starting transfers between devices, local(): z_new = lax.ppermute(u1[-1], axis_name='row', perm=xs_all)  28.1 us
    ppermute x8, waiting for transfers between devices, local(): reached = lax.ppermute(t1[-1], axis_name='row', perm=pile)  20.5 us
    dot_general x1, matrix products, attend(): jnp.einsum('qc,kc->qk', queries, key_piece, preferred_element_type=jnp.fl...  14.7 us
    ppermute x8, starting transfers between devices, local(): reached = lax.ppermute(t1[-1], axis_name='row', perm=pile)  14.6 us
    dot_general x1, matrix products, attend(): jnp.dot(expo.astype(jnp.bfloat16), value_piece, preferred_element_type=jn...  14.2 us
    reduce_sum x1, other arithmetic, attend(): denominator = jnp.sum(expo, axis=1)  8.67 us
  transfers between devices with their start and end apart: 17, of which 14 were waited for; matrix products, arithmetic and copies ran while one was open for 12% of the time, Pallas kernels for 0%

profile of v1, /device:TPU:1, one launch (start us, length us, event | category | flops | bytes accessed | tf_op | source)
XLA Modules:
  0.0 207.5 jit_solution(2291904518519642536)
XLA Ops:
  1.8 16.8 %all_to_all.12 = f32[16,1,64]{2,1,0:T(1,128)S(1)} all-to-all(f32[16,1,64]{2,1,0:T(1,128)S(1)} %broadcast_in_dim.6), channel_id=1, replica_groups=mesh['img'=16,'row'=16] {'row'}, dimensions={0} | all-to-all | bytes 8192 | tf_op jit(solution)/shard_map/all_to_all | solution.py:14
  21.1 6.1 %collective-permute-done = bf16[512,512]{1,0:T(8,128)(2,1)S(1)} collective-permute-done((bf16[512,512]{1,0:T(8,128)(2,1)S(1)}, bf16[512,512]{1,0:T(8,128)(2,1)S(1)}, u32[]{:S(2)}, u32[]{:S(2)}) %collective-permute-start) | collective-permute-done | bytes 524320 | tf_op jit(solution)/shard_map/ppermute | solution.py:107
  27.2 2.5 %collective-permute-start.1 = (bf16[512,512]{1,0:T(8,128)(2,1)S(1)}, bf16[512,512]{1,0:T(8,128)(2,1)S(1)}, u32[]{:S(2)}, u32[]{:S(2)}) collective-permute-start(bf16[512,512]{1,0:T(8,128)(2,1)S(1)} %collective-permute-done), channel_id=1, source_target_pairs={{0,1},{1,2},{2,3},{3,4},{4,5},{5,6},{6,7},{7,8},{8,9},{9,10},{10,1... | collective-permute-start | bytes 1572872 | tf_op jit(solution)/shard_map/ppermute | solution.py:107
  30.7 5.1 %collective-permute-done.1 = bf16[512,512]{1,0:T(8,128)(2,1)S(1)} collective-permute-done((bf16[512,512]{1,0:T(8,128)(2,1)S(1)}, bf16[512,512]{1,0:T(8,128)(2,1)S(1)}, u32[]{:S(2)}, u32[]{:S(2)}) %collective-permute-start.1) | collective-permute-done | bytes 524320 | tf_op jit(solution)/shard_map/ppermute | solution.py:107
  35.8 2.5 %collective-permute-start.2 = (bf16[512,512]{1,0:T(8,128)(2,1)S(1)}, bf16[512,512]{1,0:T(8,128)(2,1)S(1)}, u32[]{:S(2)}, u32[]{:S(2)}) collective-permute-start(bf16[512,512]{1,0:T(8,128)(2,1)S(1)} %collective-permute-done.1), channel_id=1, source_target_pairs={{0,1},{1,2},{2,3},{3,4},{4,5},{5,6},{6,7},{7,8},{8,9},{9,10},{10,1... | collective-permute-start | bytes 1572872 | tf_op jit(solution)/shard_map/ppermute | solution.py:107
  38.6 2.0 collective-permute-start.9
  40.6 3.9 %collective-permute-done.2 = bf16[512,512]{1,0:T(8,128)(2,1)S(1)} collective-permute-done((bf16[512,512]{1,0:T(8,128)(2,1)S(1)}, bf16[512,512]{1,0:T(8,128)(2,1)S(1)}, u32[]{:S(2)}, u32[]{:S(2)}) %collective-permute-start.2) | collective-permute-done | bytes 524320 | tf_op jit(solution)/shard_map/ppermute | solution.py:107
  44.4 2.5 %collective-permute-start.3 = (bf16[512,512]{1,0:T(8,128)(2,1)S(1)}, bf16[512,512]{1,0:T(8,128)(2,1)S(1)}, u32[]{:S(2)}, u32[]{:S(2)}) collective-permute-start(bf16[512,512]{1,0:T(8,128)(2,1)S(1)} %collective-permute-done.2), channel_id=1, source_target_pairs={{0,1},{1,2},{2,3},{3,4},{4,5},{5,6},{6,7},{7,8},{8,9},{9,10},{10,1... | collective-permute-start | bytes 1572872 | tf_op jit(solution)/shard_map/ppermute | solution.py:107
  47.5 2.9 %collective-permute-start.10 = (bf16[512,512]{1,0:T(8,128)(2,1)S(1)}, bf16[512,512]{1,0:T(8,128)(2,1)S(1)}, u32[]{:S(2)}, u32[]{:S(2)}) collective-permute-start(bf16[512,512]{1,0:T(8,128)(2,1)S(1)} %collective-permute-done.9), channel_id=1, source_target_pairs={{0,15},{1,0},{2,1},{3,2},{4,3},{5,4},{6,5},{7,6},{8,7},{9,8},{10,9... | collective-permute-start | bytes 1572872 | tf_op jit(solution)/shard_map/ppermute | solution.py:110
  50.4 2.6 %collective-permute-done.3 = bf16[512,512]{1,0:T(8,128)(2,1)S(1)} collective-permute-done((bf16[512,512]{1,0:T(8,128)(2,1)S(1)}, bf16[512,512]{1,0:T(8,128)(2,1)S(1)}, u32[]{:S(2)}, u32[]{:S(2)}) %collective-permute-start.3) | collective-permute-done | bytes 524320 | tf_op jit(solution)/shard_map/ppermute | solution.py:107
  53.0 2.5 %collective-permute-start.4 = (bf16[512,512]{1,0:T(8,128)(2,1)S(1)}, bf16[512,512]{1,0:T(8,128)(2,1)S(1)}, u32[]{:S(2)}, u32[]{:S(2)}) collective-permute-start(bf16[512,512]{1,0:T(8,128)(2,1)S(1)} %collective-permute-done.3), channel_id=1, source_target_pairs={{0,1},{1,2},{2,3},{3,4},{4,5},{5,6},{6,7},{7,8},{8,9},{9,10},{10,1... | collective-permute-start | bytes 1572872 | tf_op jit(solution)/shard_map/ppermute | solution.py:107
  56.4 3.8 %collective-permute-start.11 = (bf16[512,512]{1,0:T(8,128)(2,1)S(1)}, bf16[512,512]{1,0:T(8,128)(2,1)S(1)}, u32[]{:S(2)}, u32[]{:S(2)}) collective-permute-start(bf16[512,512]{1,0:T(8,128)(2,1)S(1)} %collective-permute-done.10), channel_id=1, source_target_pairs={{0,15},{1,0},{2,1},{3,2},{4,3},{5,4},{6,5},{7,6},{8,7},{9,8},{10,9... | collective-permute-start | bytes 1572872 | tf_op jit(solution)/shard_map/ppermute | solution.py:110
  61.6 2.5 %collective-permute-start.5 = (bf16[512,512]{1,0:T(8,128)(2,1)S(1)}, bf16[512,512]{1,0:T(8,128)(2,1)S(1)}, u32[]{:S(2)}, u32[]{:S(2)}) collective-permute-start(bf16[512,512]{1,0:T(8,128)(2,1)S(1)} %collective-permute-done.4), channel_id=1, source_target_pairs={{0,1},{1,2},{2,3},{3,4},{4,5},{5,6},{6,7},{7,8},{8,9},{9,10},{10,1... | collective-permute-start | bytes 1572872 | tf_op jit(solution)/shard_map/ppermute | solution.py:107
  66.1 4.8 %collective-permute-start.12 = (bf16[512,512]{1,0:T(8,128)(2,1)S(1)}, bf16[512,512]{1,0:T(8,128)(2,1)}, u32[]{:S(2)}, u32[]{:S(2)}) collective-permute-start(bf16[512,512]{1,0:T(8,128)(2,1)S(1)} %collective-permute-done.11), channel_id=1, source_target_pairs={{0,15},{1,0},{2,1},{3,2},{4,3},{5,4},{6,5},{7,6},{8,7},{9,8},{10,9... | collective-permute-start | bytes 1572872 | tf_op jit(solution)/shard_map/ppermute | solution.py:110
  72.7 2.3 %collective-permute-done.12 = bf16[512,512]{1,0:T(8,128)(2,1)} collective-permute-done((bf16[512,512]{1,0:T(8,128)(2,1)S(1)}, bf16[512,512]{1,0:T(8,128)(2,1)}, u32[]{:S(2)}, u32[]{:S(2)}) %collective-permute-start.12) | collective-permute-done | bytes 524320 | tf_op jit(solution)/shard_map/ppermute | solution.py:110
  75.0 5.5 %collective-permute-start.13 = (bf16[512,512]{1,0:T(8,128)(2,1)}, bf16[512,512]{1,0:T(8,128)(2,1)}, u32[]{:S(2)}, u32[]{:S(2)}) collective-permute-start(bf16[512,512]{1,0:T(8,128)(2,1)} %collective-permute-done.12), channel_id=1, source_target_pairs={{0,15},{1,0},{2,1},{3,2},{4,3},{5,4},{6,5},{7,6},{8,7},{9,8},{10,9... | collective-permute-start | bytes 1572872 | tf_op jit(solution)/shard_map/ppermute | solution.py:110
  81.5 2.4 %convolution_convert_fusion.2 = bf16[512,512]{1,0:T(8,128)(2,1)} fusion(bf16[512,512]{1,0:T(8,128)(2,1)S(1)} %fusion.41, bf16[512,512]{1,0:T(8,128)(2,1)} %param.14), kind=kOutput, calls=%fused_computation.30 | convolution fusion | flops 268697600 | bytes 1572864 | tf_op jit(solution)/shard_map/dot_general | solution.py:95
  84.2 8.0 %collective-permute-start.14 = (bf16[512,512]{1,0:T(8,128)(2,1)}, bf16[512,512]{1,0:T(8,128)(2,1)S(1)}, u32[]{:S(2)}, u32[]{:S(2)}) collective-permute-start(bf16[512,512]{1,0:T(8,128)(2,1)} %collective-permute-done.13), channel_id=1, source_target_pairs={{0,15},{1,0},{2,1},{3,2},{4,3},{5,4},{6,5},{7,6},{8,7},{9,8},{10,9... | collective-permute-start | bytes 1572872 | tf_op jit(solution)/shard_map/ppermute | solution.py:110
  92.3 1.9 constant_dynamic-update-slice_fusion.31
  96.0 1.9 constant_dynamic-update-slice_fusion.29
  101.7 1.9 constant_dynamic-update-slice_fusion.26
  116.1 1.9 constant_dynamic-update-slice_fusion.15
  118.0 1.9 constant_dynamic-update-slice_fusion.14
  129.2 1.9 constant_dynamic-update-slice_fusion.2
  131.1 1.9 constant_dynamic-update-slice_fusion.1
  133.8 14.7 %multiply_reduce_fusion = (f32[512]{0:T(512)S(1)}, f32[512,8192]{1,0:T(8,128)}) fusion(bf16[512,512]{1,0:T(8,128)(2,1)} %convolution_convert_fusion.2, bf16[512,512]{1,0:T(8,128)(2,1)S(1)} %copy-done, bf16[16384,512]{1,0:T(8,128)(2,1)} %constant_dynamic-update-slice_fusion, s32[]{:T(128)S(6)} %select_n.14), kind=kOutput, calls=%fused_computation.1 | convolution fusion | flops 8602517504 | bytes 26216452 | tf_op jit(solution)/shard_map/qc,kc->qk/dot_general | solution.py:68
  148.6 8.7 %fusion = f32[512]{0:T(512)S(1)} fusion(f32[512,8192]{1,0:T(8,128)} %get-tuple-element.24, f32[512]{0:T(512)S(1)} %broadcast_maximum_fusion), kind=kLoop, calls=%fused_computation.2 | loop fusion | flops 12582400 | bytes 16781312 | tf_op jit(solution)/shard_map/reduce_sum | solution.py:72
  157.3 14.2 %fusion.23 = bf16[512,512]{1,0:T(8,128)(2,1)S(1)} fusion(bf16[512,512]{1,0:T(8,128)(2,1)S(1)} %copy-done.17, bf16[16384,512]{1,0:T(8,128)(2,1)} %constant_dynamic-update-slice_fusion, s32[]{:T(128)S(6)} %select_n.14, f32[512,8192]{1,0:T(8,128)} %get-tuple-element.24, f32[512]{0:T(512)S(1)} %broadcast_maximum_fusion, f32[512]{0:T(512)S(1)} %fusion), kind=kOutput, calls=%fused_computation.33 | convolution fusion | flops 8607236096 | bytes 26218500 | tf_op jit(solution)/shard_map/dot_general | solution.py:73
  172.6 17.1 %all_to_all.13 = f32[16,1,64]{2,1,0:T(1,128)S(1)} all-to-all(f32[16,1,64]{2,1,0:T(1,128)S(1)} %broadcast_in_dim.8), channel_id=1, replica_groups=mesh['img'=16,'row'=16] {'row'}, dimensions={0} | all-to-all | bytes 8192 | tf_op jit(solution)/shard_map/all_to_all | solution.py:14
  190.5 2.7 %collective-permute-start.15 = (bf16[1,128,512]{2,1,0:T(8,128)(2,1)S(1)}, bf16[1,128,512]{2,1,0:T(8,128)(2,1)S(1)}, u32[]{:S(2)}, u32[]{:S(2)}) collective-permute-start(bf16[1,128,512]{2,1,0:T(8,128)(2,1)S(1)} %get-tuple-element.17), channel_id=1, source_target_pairs={{0,1},{1,2},{2,3},{3,4},{4,5},{5,6},{6,7},{7,8},{8,9},{9,10},{10,1... | collective-permute-start | bytes 393224 | tf_op jit(solution)/shard_map/ppermute | solution.py:38
  193.3 1.9 collective-permute-start.16
  195.2 4.3 %collective-permute-done.16 = bf16[1,128,512]{2,1,0:T(8,128)(2,1)S(1)} collective-permute-done((bf16[1,128,512]{2,1,0:T(8,128)(2,1)S(1)}, bf16[1,128,512]{2,1,0:T(8,128)(2,1)S(1)}, u32[]{:S(2)}, u32[]{:S(2)}) %collective-permute-start.16) | collective-permute-done | bytes 131104 | tf_op jit(solution)/shard_map/ppermute | solution.py:40
  (125 shorter events, 51.5 us)
Async XLA Ops:
  0.0 133.8 %copy-start = (bf16[512,512]{1,0:T(8,128)(2,1)S(1)}, bf16[512,512]{1,0:T(8,128)(2,1)}, u32[]{:S(2)}) copy-start(bf16[512,512]{1,0:T(8,128)(2,1)} %param.15) | copy-start | bytes 1572868
  20.2 7.0 %collective-permute-start = (bf16[512,512]{1,0:T(8,128)(2,1)S(1)}, bf16[512,512]{1,0:T(8,128)(2,1)S(1)}, u32[]{:S(2)}, u32[]{:S(2)}) collective-permute-start(bf16[512,512]{1,0:T(8,128)(2,1)S(1)} %fusion.41), channel_id=1, source_target_pairs={{0,1},{1,2},{2,3},{3,4},{4,5},{5,6},{6,7},{7,8},{8,9},{9,10},{10,1... | collective-permute-start | bytes 1572872 | tf_op jit(solution)/shard_map/ppermute | solution.py:107
  27.2 8.6 %collective-permute-start.1 = (bf16[512,512]{1,0:T(8,128)(2,1)S(1)}, bf16[512,512]{1,0:T(8,128)(2,1)S(1)}, u32[]{:S(2)}, u32[]{:S(2)}) collective-permute-start(bf16[512,512]{1,0:T(8,128)(2,1)S(1)} %collective-permute-done), channel_id=1, source_target_pairs={{0,1},{1,2},{2,3},{3,4},{4,5},{5,6},{6,7},{7,8},{8,9},{9,10},{10,1... | collective-permute-start | bytes 1572872 | tf_op jit(solution)/shard_map/ppermute | solution.py:107
  29.7 8.9 %collective-permute-start.8 = (bf16[512,512]{1,0:T(8,128)(2,1)S(1)}, bf16[512,512]{1,0:T(8,128)(2,1)S(1)}, u32[]{:S(2)}, u32[]{:S(2)}) collective-permute-start(bf16[512,512]{1,0:T(8,128)(2,1)S(1)} %fusion.41), channel_id=1, source_target_pairs={{0,15},{1,0},{2,1},{3,2},{4,3},{5,4},{6,5},{7,6},{8,7},{9,8},{10,9... | collective-permute-start | bytes 1572872 | tf_op jit(solution)/shard_map/ppermute | solution.py:110
  35.8 8.6 %collective-permute-start.2 = (bf16[512,512]{1,0:T(8,128)(2,1)S(1)}, bf16[512,512]{1,0:T(8,128)(2,1)S(1)}, u32[]{:S(2)}, u32[]{:S(2)}) collective-permute-start(bf16[512,512]{1,0:T(8,128)(2,1)S(1)} %collective-permute-done.1), channel_id=1, source_target_pairs={{0,1},{1,2},{2,3},{3,4},{4,5},{5,6},{6,7},{7,8},{8,9},{9,10},{10,1... | collective-permute-start | bytes 1572872 | tf_op jit(solution)/shard_map/ppermute | solution.py:107
  38.6 8.9 %collective-permute-start.9 = (bf16[512,512]{1,0:T(8,128)(2,1)S(1)}, bf16[512,512]{1,0:T(8,128)(2,1)S(1)}, u32[]{:S(2)}, u32[]{:S(2)}) collective-permute-start(bf16[512,512]{1,0:T(8,128)(2,1)S(1)} %collective-permute-done.8), channel_id=1, source_target_pairs={{0,15},{1,0},{2,1},{3,2},{4,3},{5,4},{6,5},{7,6},{8,7},{9,8},{10,9... | collective-permute-start | bytes 1572872 | tf_op jit(solution)/shard_map/ppermute | solution.py:110
  44.4 8.6 %collective-permute-start.3 = (bf16[512,512]{1,0:T(8,128)(2,1)S(1)}, bf16[512,512]{1,0:T(8,128)(2,1)S(1)}, u32[]{:S(2)}, u32[]{:S(2)}) collective-permute-start(bf16[512,512]{1,0:T(8,128)(2,1)S(1)} %collective-permute-done.2), channel_id=1, source_target_pairs={{0,1},{1,2},{2,3},{3,4},{4,5},{5,6},{6,7},{7,8},{8,9},{9,10},{10,1... | collective-permute-start | bytes 1572872 | tf_op jit(solution)/shard_map/ppermute | solution.py:107
  47.5 8.9 %collective-permute-start.10 = (bf16[512,512]{1,0:T(8,128)(2,1)S(1)}, bf16[512,512]{1,0:T(8,128)(2,1)S(1)}, u32[]{:S(2)}, u32[]{:S(2)}) collective-permute-start(bf16[512,512]{1,0:T(8,128)(2,1)S(1)} %collective-permute-done.9), channel_id=1, source_target_pairs={{0,15},{1,0},{2,1},{3,2},{4,3},{5,4},{6,5},{7,6},{8,7},{9,8},{10,9... | collective-permute-start | bytes 1572872 | tf_op jit(solution)/shard_map/ppermute | solution.py:110
  53.0 22.0 %copy-start.8 = (bf16[512,512]{1,0:T(8,128)(2,1)}, bf16[512,512]{1,0:T(8,128)(2,1)S(1)}, u32[]{:S(2)}) copy-start(bf16[512,512]{1,0:T(8,128)(2,1)S(1)} %collective-permute-done.3) | copy-start | bytes 1572868
  53.0 8.6 %collective-permute-start.4 = (bf16[512,512]{1,0:T(8,128)(2,1)S(1)}, bf16[512,512]{1,0:T(8,128)(2,1)S(1)}, u32[]{:S(2)}, u32[]{:S(2)}) collective-permute-start(bf16[512,512]{1,0:T(8,128)(2,1)S(1)} %collective-permute-done.3), channel_id=1, source_target_pairs={{0,1},{1,2},{2,3},{3,4},{4,5},{5,6},{6,7},{7,8},{8,9},{9,10},{10,1... | collective-permute-start | bytes 1572872 | tf_op jit(solution)/shard_map/ppermute | solution.py:107
  56.4 8.9 %collective-permute-start.11 = (bf16[512,512]{1,0:T(8,128)(2,1)S(1)}, bf16[512,512]{1,0:T(8,128)(2,1)S(1)}, u32[]{:S(2)}, u32[]{:S(2)}) collective-permute-start(bf16[512,512]{1,0:T(8,128)(2,1)S(1)} %collective-permute-done.10), channel_id=1, source_target_pairs={{0,15},{1,0},{2,1},{3,2},{4,3},{5,4},{6,5},{7,6},{8,7},{9,8},{10,9... | collective-permute-start | bytes 1572872 | tf_op jit(solution)/shard_map/ppermute | solution.py:110
  61.6 18.9 %copy-start.10 = (bf16[512,512]{1,0:T(8,128)(2,1)}, bf16[512,512]{1,0:T(8,128)(2,1)S(1)}, u32[]{:S(2)}) copy-start(bf16[512,512]{1,0:T(8,128)(2,1)S(1)} %collective-permute-done.4) | copy-start | bytes 1572868
  61.6 9.8 %collective-permute-start.5 = (bf16[512,512]{1,0:T(8,128)(2,1)S(1)}, bf16[512,512]{1,0:T(8,128)(2,1)S(1)}, u32[]{:S(2)}, u32[]{:S(2)}) collective-permute-start(bf16[512,512]{1,0:T(8,128)(2,1)S(1)} %collective-permute-done.4), channel_id=1, source_target_pairs={{0,1},{1,2},{2,3},{3,4},{4,5},{5,6},{6,7},{7,8},{8,9},{9,10},{10,1... | collective-permute-start | bytes 1572872 | tf_op jit(solution)/shard_map/ppermute | solution.py:107
  66.1 8.9 %collective-permute-start.12 = (bf16[512,512]{1,0:T(8,128)(2,1)S(1)}, bf16[512,512]{1,0:T(8,128)(2,1)}, u32[]{:S(2)}, u32[]{:S(2)}) collective-permute-start(bf16[512,512]{1,0:T(8,128)(2,1)S(1)} %collective-permute-done.11), channel_id=1, source_target_pairs={{0,15},{1,0},{2,1},{3,2},{4,3},{5,4},{6,5},{7,6},{8,7},{9,8},{10,9... | collective-permute-start | bytes 1572872 | tf_op jit(solution)/shard_map/ppermute | solution.py:110
  71.4 9.9 %collective-permute-start.6 = (bf16[512,512]{1,0:T(8,128)(2,1)S(1)}, bf16[512,512]{1,0:T(8,128)(2,1)}, u32[]{:S(2)}, u32[]{:S(2)}) collective-permute-start(bf16[512,512]{1,0:T(8,128)(2,1)S(1)} %collective-permute-done.5), channel_id=1, source_target_pairs={{0,1},{1,2},{2,3},{3,4},{4,5},{5,6},{6,7},{7,8},{8,9},{9,10},{10,1... | collective-permute-start | bytes 1572872 | tf_op jit(solution)/shard_map/ppermute | solution.py:107
  75.0 9.2 %collective-permute-start.13 = (bf16[512,512]{1,0:T(8,128)(2,1)}, bf16[512,512]{1,0:T(8,128)(2,1)}, u32[]{:S(2)}, u32[]{:S(2)}) collective-permute-start(bf16[512,512]{1,0:T(8,128)(2,1)} %collective-permute-done.12), channel_id=1, source_target_pairs={{0,15},{1,0},{2,1},{3,2},{4,3},{5,4},{6,5},{7,6},{8,7},{9,8},{10,9... | collective-permute-start | bytes 1572872 | tf_op jit(solution)/shard_map/ppermute | solution.py:110
  81.4 10.9 %collective-permute-start.7 = (bf16[512,512]{1,0:T(8,128)(2,1)}, bf16[512,512]{1,0:T(8,128)(2,1)}, u32[]{:S(2)}, u32[]{:S(2)}) collective-permute-start(bf16[512,512]{1,0:T(8,128)(2,1)} %collective-permute-done.6), channel_id=1, source_target_pairs={{0,1},{1,2},{2,3},{3,4},{4,5},{5,6},{6,7},{7,8},{8,9},{9,10},{10,1... | collective-permute-start | bytes 1572872 | tf_op jit(solution)/shard_map/ppermute | solution.py:107
  81.4 38.5 %copy-start.13 = (bf16[512,512]{1,0:T(8,128)(2,1)S(1)}, bf16[512,512]{1,0:T(8,128)(2,1)}, u32[]{:S(2)}) copy-start(bf16[512,512]{1,0:T(8,128)(2,1)} %copy-done.12) | copy-start | bytes 1572868
  81.4 39.3 %copy-start.11 = (bf16[512,512]{1,0:T(8,128)(2,1)S(1)}, bf16[512,512]{1,0:T(8,128)(2,1)}, u32[]{:S(2)}) copy-start(bf16[512,512]{1,0:T(8,128)(2,1)} %copy-done.10) | copy-start | bytes 1572868
  81.4 40.2 %copy-start.9 = (bf16[512,512]{1,0:T(8,128)(2,1)S(1)}, bf16[512,512]{1,0:T(8,128)(2,1)}, u32[]{:S(2)}) copy-start(bf16[512,512]{1,0:T(8,128)(2,1)} %copy-done.8) | copy-start | bytes 1572868
  81.4 41.0 %copy-start.3 = (bf16[512,512]{1,0:T(8,128)(2,1)S(1)}, bf16[512,512]{1,0:T(8,128)(2,1)}, u32[]{:S(2)}) copy-start(bf16[512,512]{1,0:T(8,128)(2,1)} %copy-done.2) | copy-start | bytes 1572868
  81.4 46.1 %copy-start.5 = (bf16[512,512]{1,0:T(8,128)(2,1)S(1)}, bf16[512,512]{1,0:T(8,128)(2,1)}, u32[]{:S(2)}) copy-start(bf16[512,512]{1,0:T(8,128)(2,1)} %copy-done.4) | copy-start | bytes 1572868
  81.5 46.9 %copy-start.7 = (bf16[512,512]{1,0:T(8,128)(2,1)S(1)}, bf16[512,512]{1,0:T(8,128)(2,1)}, u32[]{:S(2)}) copy-start(bf16[512,512]{1,0:T(8,128)(2,1)} %copy-done.6) | copy-start | bytes 1572868
  84.2 31.0 %collective-permute-start.14 = (bf16[512,512]{1,0:T(8,128)(2,1)}, bf16[512,512]{1,0:T(8,128)(2,1)S(1)}, u32[]{:S(2)}, u32[]{:S(2)}) collective-permute-start(bf16[512,512]{1,0:T(8,128)(2,1)} %collective-permute-done.13), channel_id=1, source_target_pairs={{0,15},{1,0},{2,1},{3,2},{4,3},{5,4},{6,5},{7,6},{8,7},{9,8},{10,9... | collective-permute-start | bytes 1572872 | tf_op jit(solution)/shard_map/ppermute | solution.py:110
  157.3 14.3 %copy-start.1 = (bf16[4,128,512]{2,1,0:T(8,128)(2,1)S(1)}, bf16[4,128,512]{2,1,0:T(8,128)(2,1)}, u32[]{:S(2)}) copy-start(bf16[4,128,512]{2,1,0:T(8,128)(2,1)} %param.11) | copy-start | bytes 1572868
  157.3 14.3 %copy-start.18 = (bf16[512,512]{1,0:T(8,128)(2,1)S(1)}, bf16[512,512]{1,0:T(8,128)(2,1)}, u32[]{:S(2)}) copy-start(bf16[512,512]{1,0:T(8,128)(2,1)} %param.17) | copy-start | bytes 1572868
  157.3 32.8 %copy-start.14 = (f32[512]{0:T(512)S(1)}, f32[512]{0:T(512)}, u32[]{:S(2)}) copy-start(f32[512]{0:T(512)} %param.19) | copy-start | bytes 6148
  157.3 32.8 %copy-start.15 = (f32[512]{0:T(512)S(1)}, f32[512]{0:T(512)}, u32[]{:S(2)}) copy-start(f32[512]{0:T(512)} %param.18) | copy-start | bytes 6148
  171.6 31.9 %slice-start = ((s8[4718592]{0:T(1024)(128)(4,1)}), s8[524288]{0:T(1024)(128)(4,1)S(1)}, s32[]{:S(2)}) async-start(s8[4718592]{0:T(1024)(128)(4,1)} %bitcast.72), calls=%async_computation.2 | async-start | bytes 1048576
  190.5 15.7 %copy-start.16 = (f32[512]{0:T(512)S(1)}, f32[512]{0:T(512)}, u32[]{:S(2)}) copy-start(f32[512]{0:T(512)} %param.21) | copy-start | bytes 6148
  190.5 4.7 %collective-permute-start.15 = (bf16[1,128,512]{2,1,0:T(8,128)(2,1)S(1)}, bf16[1,128,512]{2,1,0:T(8,128)(2,1)S(1)}, u32[]{:S(2)}, u32[]{:S(2)}) collective-permute-start(bf16[1,128,512]{2,1,0:T(8,128)(2,1)S(1)} %get-tuple-element.17), channel_id=1, source_target_pairs={{0,1},{1,2},{2,3},{3,4},{4,5},{5,6},{6,7},{7,8},{8,9},{9,10},{10,1... | collective-permute-start | bytes 393224 | tf_op jit(solution)/shard_map/ppermute | solution.py:38
  193.3 6.3 %collective-permute-start.16 = (bf16[1,128,512]{2,1,0:T(8,128)(2,1)S(1)}, bf16[1,128,512]{2,1,0:T(8,128)(2,1)S(1)}, u32[]{:S(2)}, u32[]{:S(2)}) collective-permute-start(bf16[1,128,512]{2,1,0:T(8,128)(2,1)S(1)} %get-tuple-element.18), channel_id=1, source_target_pairs={{1,0},{2,1},{3,2},{4,3},{5,4},{6,5},{7,6},{8,7},{9,8},{10,9},{11,1... | collective-permute-start | bytes 393224 | tf_op jit(solution)/shard_map/ppermute | solution.py:40
  (6 other events, 39.0 us)
